TPU v7x, 256 devices: a whole 4x4x8 slice. The times are simulated.
256 devices in a mesh: slab: 32 (over z, y), energy: 8 (over x, core).
Axes of the slice: x: 4, y: 4, z: 8, core: 2. Of those that a mesh axis runs over, the one named last changes fastest.
Arguments:
- green: bfloat16 [8, 32, 3, 2, 384, 384], P('energy', 'slab'), may hold values from -0.3125 to 0.3125
- sigma: bfloat16 [8, 32, 3, 2, 384, 384], P('energy', 'slab'), may hold values from -4 to 4
- phonon: bfloat16 [8, 32, 2, 384, 384], P('energy', 'slab'), may hold values from -4 to 4
- pair_off: int32 [32, 3], replicated, may hold values from -2 to 2, as said below
- pair_count: int32 [32], replicated, may hold values from 1 to 3, as said below
- pair_range: int32 [32, 3], replicated, may hold values from 96 to 384, as said below
Outputs:
- lesser: float32 [8, 32, 2, 384, 384], P('energy', 'slab')
Inputs may be any that keep to these rules, and one draw needn't show every extreme that they name: The partner slab k + pair_off[k, q] lies inside the grid. `pair_count`: some slab has 3 live slots. `pair_range`: a multiple of 96; some pair couples all 384 orbitals.
All inputs are finite; a program needn't handle non-finite values.
Results may differ from a plain program's by a relative error of at most 0.0035.
Values may be sent and summed in bfloat16 or wider, within the bound.
A program may use at most 64 MiB of HBM per device.

v0:
```python
import functools

import jax
import jax.numpy as jnp
from jax import lax
from jax.experimental import pallas as pl
from jax.experimental.pallas import tpu as pltpu
from jax.sharding import PartitionSpec as P

MESH = pl.DeviceIdType.MESH
F32 = jnp.float32
BF16 = jnp.bfloat16
TILE = 16
CHUNK = 128
UNIT = 96
GROUP = 6
LIST = 24
DIRECT = 18
HOP = 4
OFFSETS = (1, 2, -1, -2)


def extent(reach):
    steps = [(reach >= n * UNIT).astype(jnp.int32) for n in range(1, 5)]
    down = steps[0] + steps[1] + steps[2] + steps[3]
    across = steps[0] + steps[1] + steps[2]
    return down, across, down * across


def crowded_kernel(off_ref, count_ref, range_ref, out_ref):
    off, reach = off_ref[...], range_ref[...]
    slots, slabs = off.shape
    live = lax.broadcasted_iota(jnp.int32, off.shape, 0) < count_ref[...]
    place = lax.broadcasted_iota(jnp.int32, (1, slabs), 1) % HOP
    crowded = jnp.zeros((1, slabs), F32)
    for way in range(2):
        filled = jnp.zeros((1, slabs), jnp.int32)
        for offset in OFFSETS[2 * way : 2 * way + 2]:
            widest = jnp.max(jnp.where(live & (off == offset), reach, 0), axis=0, keepdims=True)
            filled = filled + extent(widest)[2]
        above = jnp.concatenate([filled[:, HOP:], filled[:, :HOP]], axis=1)
        below = jnp.concatenate([filled[:, -HOP:], filled[:, :-HOP]], axis=1)
        relay = jnp.where(place == HOP - 1, below, above) if way == 0 else jnp.where(place == 0, above, below)
        crowded = crowded + ((filled > DIRECT) & (relay > LIST - 2 * GROUP)).astype(F32)
    out_ref[0] = jnp.max(crowded).astype(jnp.int32)


def kernel(
    slabs,
    energies,
    around,
    off_hbm,
    count_hbm,
    range_hbm,
    green_hbm,
    sigma_hbm,
    phonon_hbm,
    out_ref,
    off_ref,
    count_ref,
    range_ref,
    green_v,
    sigma_v,
    near_v,
    mine_v,
    own_v,
    list_v,
    from_left_v,
    from_right_v,
    spill_v,
    cent_v,
    block_v,
    b_v,
    a_v,
    y_v,
    part_v,
    acc_v,
    local_sem,
    near_send,
    near_recv,
    unit_send,
    unit_recv,
    spill_send,
    spill_recv,
    back_send,
    back_recv,
    cent_send,
    cent_recv,
):
    k = lax.axis_index("slab")
    e = lax.axis_index("energy")
    width = green_v.shape[-1]
    slots = sigma_v.shape[0]
    chunks = width // CHUNK
    has_low, has_high = e > 0, e < energies - 1

    def ring(slab):
        return lax.rem(slab + slabs, slabs)

    next_k, last_k = ring(k + 1), ring(k - 1)

    tables = [
        pltpu.make_async_copy(source, held, local_sem.at[n])
        for n, (source, held) in enumerate(
            ((off_hbm, off_ref), (count_hbm, count_ref), (range_hbm, range_ref))
        )
    ]
    load_sigma = pltpu.make_async_copy(sigma_hbm.at[0, 0], sigma_v, local_sem.at[3])
    load_green = pltpu.make_async_copy(green_hbm.at[0, 0], green_v, local_sem.at[4])
    for table in tables:
        table.start()
    load_sigma.start()

    barrier = pltpu.get_barrier_semaphore()
    always = [next_k, last_k] + ([ring(k + HOP), ring(k - HOP)] if around else [])
    for slab in always:
        pl.semaphore_signal(barrier, inc=1, device_id={"slab": slab}, device_id_type=MESH)
    for there, energy in ((has_low, e - 1), (has_high, e + 1)):

        @pl.when(there)
        def _():
            pl.semaphore_signal(barrier, inc=1, device_id={"energy": energy}, device_id_type=MESH)

    peers = len(always) + 2 - sum((e == end).astype(jnp.int32) for end in (0, energies - 1))
    pl.semaphore_wait(barrier, peers)

    def near_copy(slot, target):
        return pltpu.make_async_remote_copy(
            src_ref=phonon_hbm.at[0, 0],
            dst_ref=near_v.at[slot],
            send_sem=near_send.at[slot],
            recv_sem=near_recv.at[slot],
            device_id={"energy": target},
            device_id_type=MESH,
        )

    up, down = near_copy(0, e + 1), near_copy(1, e - 1)

    @pl.when(has_high)
    def _():
        up.start()

    @pl.when(has_low)
    def _():
        down.start()

    def remote(source, target, sent, received, slab):
        return pltpu.make_async_remote_copy(
            src_ref=source,
            dst_ref=target,
            send_sem=sent,
            recv_sem=received,
            device_id={"slab": slab},
            device_id_type=MESH,
        )

    place = lax.rem(k, HOP)
    turn = (jnp.where(place == HOP - 1, -HOP, HOP), jnp.where(place == 0, HOP, -HOP))
    back = (jnp.where(place == 0, HOP, -HOP), jnp.where(place == HOP - 1, -HOP, HOP))
    beside = (next_k, last_k)
    got_v = (from_left_v, from_right_v)
    groups = (DIRECT if around else LIST) // GROUP
    direct, spill, returned, centre = [], [], [], []
    pieces = [(slice(None), c * CHUNK) for c in range(chunks - 1)]
    pieces += [(slice(c, c + 1), width - CHUNK) for c in range(chunks)]
    for way in range(2):
        direct.append([])
        for g in range(groups):
            units = slice(g * GROUP, (g + 1) * GROUP)
            direct[way].append(
                remote(
                    list_v.at[way, units],
                    got_v[way].at[units],
                    unit_send.at[way, g],
                    unit_recv.at[way, g],
                    beside[way],
                )
            )
        spill.append(
            remote(
                list_v.at[way, DIRECT:LIST],
                spill_v.at[way],
                spill_send.at[way],
                spill_recv.at[way],
                ring(k + turn[way]),
            )
        )
        returned.append(
            remote(
                got_v[way].at[DIRECT - GROUP : DIRECT],
                got_v[way].at[DIRECT:LIST],
                back_send.at[way],
                back_recv.at[way],
                ring(k + back[way]),
            )
        )
        centre.append([])
        for n, (these, row) in enumerate(pieces):
            centre[way].append(
                remote(
                    own_v.at[these, row : row + CHUNK],
                    cent_v.at[way, these, row : row + CHUNK],
                    cent_send.at[way, n],
                    cent_recv.at[way, n],
                    beside[way],
                )
            )

    def live_reach(slab, q, offset):
        live = (q < count_ref[slab]) & (off_ref[q, slab] == offset)
        return jnp.where(live, range_ref[q, slab], 0)

    def combine(wanted, with_phonon):
        reach = [[live_reach(k, q, offset) for q in range(slots)] for _, offset in wanted]

        def step(t, carry):
            rows = pl.ds(pl.multiple_of(t * TILE, TILE), TILE)
            row_ids = t * TILE + lax.broadcasted_iota(jnp.int32, (TILE, width), 0)
            col_ids = lax.broadcasted_iota(jnp.int32, (TILE, width), 1)
            far = jnp.maximum(row_ids, col_ids)
            m = lax.div(t, UNIT // TILE)
            unit_rows = pl.ds(pl.multiple_of(t * TILE - m * UNIT, TILE), TILE)
            for part in range(2):
                terms = [sigma_v[q, part, rows, :].astype(F32) for q in range(slots)]
                for n, (at, _) in enumerate(wanted):
                    kept = [jnp.where(far < reach[n][q], terms[q], 0.0) for q in range(slots)]
                    total = functools.reduce(jnp.add, kept)
                    if with_phonon:
                        low = near_v[0, part, rows, :].astype(F32)
                        high = near_v[1, part, rows, :].astype(F32)
                        total = total + (0.5 * (low + high)).astype(BF16).astype(F32)
                    total = total.astype(BF16)
                    lanes = slice(part * CHUNK, (part + 1) * CHUNK)
                    for c in range(chunks):
                        value = total[:, c * CHUNK : (c + 1) * CHUNK]
                        if with_phonon:
                            own_v[c, rows, lanes] = value
                        else:
                            mine_v[at, m, c, unit_rows, lanes] = value
            return carry

        lax.fori_loop(0, width // TILE, step, 0)

    def layout(slab, way):
        blocks = []
        for offset in OFFSETS[2 * way : 2 * way + 2]:
            reach = functools.reduce(jnp.maximum, [live_reach(slab, q, offset) for q in range(slots)])
            blocks.append(extent(reach))
        return blocks

    def pack(way, first, last):
        (_, across_a, size_a), (_, across_b, size_b) = layout(k, way)

        def step(p, carry):
            in_a = p < size_a
            unit = jnp.where(in_a, p, jnp.maximum(p - size_a, 0))
            across = jnp.where(in_a, across_a, across_b)
            row = jnp.where(across == 3, lax.div(unit, 3), jnp.where(across == 2, lax.div(unit, 2), unit))
            col = jnp.clip(unit - row * across, 0, chunks - 1)
            row = jnp.clip(row, 0, width // UNIT - 1)
            at = 2 * way + jnp.where(in_a, 0, 1)
            keep = jnp.where(p < size_a + size_b, 1.0, 0.0).astype(BF16)
            list_v[way, p] = mine_v[at, row, col] * keep
            return carry

        lax.fori_loop(first, last, step, 0)

    for table in tables:
        table.wait()
    load_sigma.wait()
    load_green.start()
    held_back = groups - 1 if around else groups
    for way in range(2):
        combine([(2 * way + n, OFFSETS[2 * way + n]) for n in range(2)], False)
        if around:
            pack(way, DIRECT, LIST)
            spill[way].start()
            pack(way, 0, DIRECT)
        else:
            pack(way, 0, LIST)
        for copy in direct[way][:held_back]:
            copy.start()

    for there, slot in ((has_low, 0), (has_high, 1)):

        @pl.when(jnp.logical_not(there))
        def _():
            near_v[slot] = jnp.zeros_like(near_v[slot])

    @pl.when(has_low)
    def _():
        up.wait_recv()

    @pl.when(has_high)
    def _():
        down.wait_recv()

    combine([(4, 0)], True)
    if around:
        for way in range(2):
            spill[way].wait_recv()
            for j in range(GROUP):
                p = DIRECT - GROUP + j
                list_v[way, p] = list_v[way, p] + spill_v[way, j]
        for way in range(2):
            direct[way][-1].start()
    for way in range(2):
        for copy in centre[way]:
            copy.start()

    load_green.wait()
    for at in range(3):
        for part in range(2):
            turned = green_v[at, part].astype(F32).T
            plain = turned.astype(BF16)
            minus = (-turned).astype(BF16)
            for c in range(chunks):
                source = slice(c * CHUNK, (c + 1) * CHUNK)
                real = slice(2 * c * CHUNK, (2 * c + 1) * CHUNK)
                imag = slice((2 * c + 1) * CHUNK, (2 * c + 2) * CHUNK)
                if part == 0:
                    b_v[at, real, :width] = plain[source]
                    b_v[at, imag, width:] = plain[source]
                else:
                    b_v[at, real, width:] = minus[source]
                    b_v[at, imag, :width] = plain[source]
    inside = (None, k > 0, k < slabs - 1)
    for c in range(chunks):
        for n, at in enumerate((1, 0, 2)):
            for part in range(2):
                to = n * 2 * CHUNK + part * CHUNK
                value = green_v[at, part, :, c * CHUNK : (c + 1) * CHUNK]
                if inside[n] is not None:
                    value = jnp.where(inside[n], value, jnp.zeros_like(value))
                a_v[c, :, to : to + CHUNK] = value

    def dot(a, b):
        return jnp.dot(a, b, preferred_element_type=F32)

    def b_chunk(at, c):
        return b_v[at, 2 * c * CHUNK : 2 * (c + 1) * CHUNK]

    def put(at, x):
        real = x[:, :width].astype(BF16)
        imag = x[:, width:].astype(BF16)
        y_v[at : at + CHUNK, :width] = real
        y_v[at : at + CHUNK, width:] = imag
        y_v[at + CHUNK : at + 2 * CHUNK, :width] = -imag
        y_v[at + CHUNK : at + 2 * CHUNK, width:] = real

    for n, (at, partner) in enumerate(((2, 0), (0, 2))):
        for r in range(2):
            rows = slice(r * width // 2, (r + 1) * width // 2)
            units = slice(rows.start // UNIT, rows.stop // UNIT)
            x = None
            for c in range(chunks):
                term = dot(mine_v[at, units, c].reshape(width // 2, 2 * CHUNK), b_chunk(partner, c))
                x = term if x is None else x + term
            part_v[0, rows] = x if n == 0 else part_v[0, rows] + x
    for r in range(chunks):
        rows = slice(r * CHUNK, (r + 1) * CHUNK)
        x = part_v[0, rows]
        for c in range(chunks):
            x = x + dot(own_v[c, rows], b_chunk(1, c))
        put(0, x)
        term = dot(a_v[r, :, : 2 * CHUNK], y_v[: 2 * CHUNK])
        acc_v[...] = term if r == 0 else acc_v[...] + term

    if around:
        for way in range(2):
            direct[way][-1].wait_recv()
            returned[way].start()

    for way in range(2):
        for copy in direct[way][:held_back]:
            copy.wait_recv()
        if around:
            returned[way].wait_recv()
        start = 0
        blocks = layout((last_k, next_k)[way], way)
        for n, (down_n, across_n, size_n) in enumerate(blocks):
            for m in range(width // UNIT):
                for c in range(chunks):
                    position = jnp.clip(start + m * across_n + c, 0, LIST - 1)
                    keep = jnp.where((m < down_n) & (c < across_n), 1.0, 0.0).astype(BF16)
                    block_v[c, m * UNIT : (m + 1) * UNIT] = got_v[way][position] * keep
            start = start + size_n
            partner = ((1, 2), (1, 0))[way][n]
            for r in range(chunks):
                rows = slice(r * CHUNK, (r + 1) * CHUNK)
                x = None
                for c in range(chunks):
                    term = dot(block_v[c, rows], b_chunk(partner, c))
                    x = term if x is None else x + term
                part_v[way, rows] = x if n == 0 else part_v[way, rows] + x

    for n, (these, row) in enumerate(pieces):
        rows = slice(row, row + CHUNK)
        final = n == len(pieces) - 1
        for way in range(2):
            centre[way][n].wait_recv()
            partner = (0, 2)[way]
            x = part_v[way, rows]
            for c in range(chunks)[these]:
                x = x + dot(cent_v[way, c, rows], b_chunk(partner, c))
            if n < chunks - 1 or final:
                put(2 * CHUNK * way, x)
            else:
                part_v[way, rows] = x
        if n < chunks - 1:
            acc_v[...] = acc_v[...] + dot(a_v[n, :, 2 * CHUNK :], y_v[...])
    for m in range(chunks):
        rows = slice(m * CHUNK, (m + 1) * CHUNK)
        total = acc_v[rows] + dot(a_v[chunks - 1, rows, 2 * CHUNK :], y_v[...])
        for part in range(2):
            out_ref[0, 0, part, rows] = total[:, part * width : (part + 1) * width]

    @pl.when(has_high)
    def _():
        up.wait_send()

    @pl.when(has_low)
    def _():
        down.wait_send()

    for way in range(2):
        for copy in direct[way] + centre[way] + ([spill[way], returned[way]] if around else []):
            copy.wait_send()


def solution(mesh):
    slabs, energies = mesh.shape["slab"], mesh.shape["energy"]

    def body(green, sigma, phonon, pair_off, pair_count, pair_range):
        width = green.shape[-1]
        slots = sigma.shape[2]
        chunks = width // CHUNK
        hbm = pl.BlockSpec(memory_space=pltpu.HBM)
        vmem = pl.BlockSpec(memory_space=pltpu.VMEM)
        split = (chunks, width, 2 * CHUNK)
        unit = (UNIT, 2 * CHUNK)
        operands = (pair_off.T, pair_count, pair_range.T, green, sigma, phonon)
        operands = [pltpu.with_memory_space_constraint(v, pltpu.HBM) for v in operands]

        def call(around, *operands):
            return pl.pallas_call(
                functools.partial(kernel, slabs, energies, around),
                out_shape=jax.ShapeDtypeStruct((1, 1, 2, width, width), F32),
                in_specs=[hbm] * 6,
                out_specs=vmem,
                scratch_shapes=[
                    pltpu.SMEM((slots, slabs), jnp.int32),
                    pltpu.SMEM((slabs,), jnp.int32),
                    pltpu.SMEM((slots, slabs), jnp.int32),
                    pltpu.VMEM((3, 2, width, width), BF16),
                    pltpu.VMEM((slots, 2, width, width), BF16),
                    pltpu.VMEM((2, 2, width, width), BF16),
                    pltpu.VMEM((4, width // UNIT, chunks) + unit, BF16),
                    pltpu.VMEM(split, BF16),
                    pltpu.VMEM((2, LIST) + unit, BF16),
                    pltpu.VMEM((LIST,) + unit, BF16),
                    pltpu.VMEM((LIST,) + unit, BF16),
                    pltpu.VMEM((2, GROUP) + unit, BF16),
                    pltpu.VMEM((2,) + split, BF16),
                    pltpu.VMEM(split, BF16),
                    pltpu.VMEM((3, 2 * width, 2 * width), BF16),
                    pltpu.VMEM((chunks, width, 6 * CHUNK), BF16),
                    pltpu.VMEM((4 * CHUNK, 2 * width), BF16),
                    pltpu.VMEM((2, width, 2 * width), F32),
                    pltpu.VMEM((width, 2 * width), F32),
                    pltpu.SemaphoreType.DMA((5,)),
                    pltpu.SemaphoreType.DMA((2,)),
                    pltpu.SemaphoreType.DMA((2,)),
                    pltpu.SemaphoreType.DMA((2, LIST // GROUP)),
                    pltpu.SemaphoreType.DMA((2, LIST // GROUP)),
                    pltpu.SemaphoreType.DMA((2,)),
                    pltpu.SemaphoreType.DMA((2,)),
                    pltpu.SemaphoreType.DMA((2,)),
                    pltpu.SemaphoreType.DMA((2,)),
                    pltpu.SemaphoreType.DMA((2, 2 * chunks - 1)),
                    pltpu.SemaphoreType.DMA((2, 2 * chunks - 1)),
                ],
                compiler_params=pltpu.CompilerParams(
                    collective_id=int(around), has_side_effects=True, vmem_limit_bytes=48 * 1024 * 1024
                ),
                name="around" if around else "straight",
            )(*operands)

        crowded = pl.pallas_call(
            crowded_kernel,
            out_shape=jax.ShapeDtypeStruct((1,), jnp.int32),
            in_specs=[vmem] * 3,
            out_specs=pl.BlockSpec(memory_space=pltpu.SMEM),
            name="crowded",
        )(pair_off.T, pair_count[None], pair_range.T)
        return lax.cond(
            crowded[0] > 0, functools.partial(call, False), functools.partial(call, True), *operands
        )

    wide = P("energy", "slab", None, None, None, None)
    slim = P("energy", "slab", None, None, None)
    return jax.shard_map(
        body,
        mesh=mesh,
        in_specs=(wide, wide, slim, P(), P(), P()),
        out_specs=slim,
        check_vma=False,
    )
```

profile of v0, /device:TPU:2, one launch (start us, length us, event | category | flops | bytes accessed | tf_op | source)
XLA Modules:
  0.0 55.8 jit_solution(8383983917671494789)
XLA Ops:
  0.0 1.4 %crowded.1 = s32[1]{0:T(128)} custom-call(s32[3,32]{1,0:T(4,128)} %bitcast.4, s32[1,32]{1,0:T(1,128)} %bitcast.10, s32[3,32]{1,0:T(4,128)} %bitcast.7), custom_call_target="tpu_custom_call" | custom-call | tf_op jit(solution)/shard_map/crowded/pallas_call | solution.py:489
  2.1 52.7 %conditional.1 = (f32[1,1,2,384,384]{4,3,2,1,0:T(8,128)S(1)}) conditional(s32[]{:T(128)} %bitcast.3, (s32[3,32]{1,0:T(4,128)}, s32[32]{0:T(128)}, s32[3,32]{1,0:T(4,128)}, bf16[1,1,3,2,384,384]{5,4,3,2,1,0:T(8,128)(2,1)}, bf16[1,1,3,2,384,384]{5,4,3,2,1,0:T(8,128)(2,1)}, /*index=5*/bf16[1,1,2,384,384]{4,3,2,1,0:T(8,128)(2,1)}) %tuple.18, ...), branch_computations={%region_0.0_spmd, %region_1.0_spmd} | conditional | bytes 8 | solution.py:496
  2.1 52.4 %around.1 = f32[1,1,2,384,384]{4,3,2,1,0:T(8,128)S(1)} custom-call(s32[3,32]{1,0:T(4,128)} %get-tuple-element.32.off_hbm, s32[32]{0:T(128)} %get-tuple-element.33.count_hbm, s32[3,32]{1,0:T(4,128)} %get-tuple-element.34.range_hbm, bf16[1,1,3,2,384,384]{5,4,3,2,1,0:T(8,128)(2,1)} %get-tuple-element.35.green_hbm, ...), custom_call_target="tpu_custom_call" | custom-call | tf_op jit(solution)/shard_map/cond/branch_0_fun/around/pallas_call | solution.py:446
  54.8 1.0 %copy.12 = f32[1,1,2,384,384]{4,3,2,1,0:T(8,128)} copy(f32[1,1,2,384,384]{4,3,2,1,0:T(8,128)S(1)} %get-tuple-element.44) | data formatting | bytes 2359296
where the time goes:
time: 55.9 us; the launch traced here: 55.8 us
  Pallas kernels  53.9 us (96%)
  local copies, waits for them, and re-layouts  1.02 us (2%)
  between operations  0.67 us (1%)
    pallas_call x1, Pallas kernels, call(): pl.pallas_call(functools.partial(kernel, slabs, energies, around), out_sh...  52.4 us
    pallas_call x1, Pallas kernels, body(): pl.pallas_call(crowded_kernel, out_shape=jax.ShapeDtypeStruct((1,), jnp.i...  1.44 us

commit v1 on v0

--- a/solution.py
+++ b/solution.py
@@ -27,11 +27,30 @@
     return down, across, down * across
 
 
+def turned(slab, way):
+    place = lax.rem(slab, HOP)
+    paired = jnp.where(lax.rem(lax.div(slab, HOP), 2) == 0, HOP, -HOP)
+    if way == 0:
+        return jnp.where(place == HOP - 1, -HOP, jnp.where(place == 1, paired, HOP))
+    return jnp.where(place == 0, HOP, jnp.where(place == 2, paired, -HOP))
+
+
+def detours(slab, way, slabs):
+    low, high = (0, slabs - 2) if way == 0 else (1, slabs - 1)
+    relay = slab + turned(slab, way)
+    return (slab >= low) & (slab <= high) & (relay >= low) & (relay <= high)
+
+
+def relayed(relay, way):
+    turn = turned(relay, way)
+    return relay + jnp.where(lax.rem(relay, HOP) == 1 + way, turn, -turn)
+
+
 def crowded_kernel(off_ref, count_ref, range_ref, out_ref):
     off, reach = off_ref[...], range_ref[...]
     slots, slabs = off.shape
     live = lax.broadcasted_iota(jnp.int32, off.shape, 0) < count_ref[...]
-    place = lax.broadcasted_iota(jnp.int32, (1, slabs), 1) % HOP
+    slab = lax.broadcasted_iota(jnp.int32, (1, slabs), 1)
     crowded = jnp.zeros((1, slabs), F32)
     for way in range(2):
         filled = jnp.zeros((1, slabs), jnp.int32)
@@ -40,8 +59,9 @@
             filled = filled + extent(widest)[2]
         above = jnp.concatenate([filled[:, HOP:], filled[:, :HOP]], axis=1)
         below = jnp.concatenate([filled[:, -HOP:], filled[:, :-HOP]], axis=1)
-        relay = jnp.where(place == HOP - 1, below, above) if way == 0 else jnp.where(place == 0, above, below)
-        crowded = crowded + ((filled > DIRECT) & (relay > LIST - 2 * GROUP)).astype(F32)
+        relay = jnp.where(turned(slab, way) > 0, above, below)
+        stuck = (relay > LIST - 2 * GROUP) | jnp.logical_not(detours(slab, way, slabs))
+        crowded = crowded + ((filled > DIRECT) & stuck).astype(F32)
     out_ref[0] = jnp.max(crowded).astype(jnp.int32)
 
 
@@ -94,10 +114,7 @@
     chunks = width // CHUNK
     has_low, has_high = e > 0, e < energies - 1
 
-    def ring(slab):
-        return lax.rem(slab + slabs, slabs)
-
-    next_k, last_k = ring(k + 1), ring(k - 1)
+    has_left, has_right = k > 0, k < slabs - 1
 
     tables = [
         pltpu.make_async_copy(source, held, local_sem.at[n])
@@ -105,24 +122,36 @@
             ((off_hbm, off_ref), (count_hbm, count_ref), (range_hbm, range_ref))
         )
     ]
-    load_sigma = pltpu.make_async_copy(sigma_hbm.at[0, 0], sigma_v, local_sem.at[3])
-    load_green = pltpu.make_async_copy(green_hbm.at[0, 0], green_v, local_sem.at[4])
+    load_sigma = []
+    for c in range(chunks):
+        rows = slice(c * CHUNK, (c + 1) * CHUNK)
+        load_sigma.append(
+            pltpu.make_async_copy(
+                sigma_hbm.at[0, 0, :, :, rows], sigma_v.at[:, :, rows], local_sem.at[4 + c]
+            )
+        )
+    load_green = pltpu.make_async_copy(green_hbm.at[0, 0], green_v, local_sem.at[3])
     for table in tables:
         table.start()
-    load_sigma.start()
+    for load in load_sigma:
+        load.start()
 
     barrier = pltpu.get_barrier_semaphore()
-    always = [next_k, last_k] + ([ring(k + HOP), ring(k - HOP)] if around else [])
-    for slab in always:
-        pl.semaphore_signal(barrier, inc=1, device_id={"slab": slab}, device_id_type=MESH)
-    for there, energy in ((has_low, e - 1), (has_high, e + 1)):
+    peers = [
+        (has_left, {"slab": k - 1}),
+        (has_right, {"slab": k + 1}),
+        (has_low, {"energy": e - 1}),
+        (has_high, {"energy": e + 1}),
+    ]
+    if around:
+        peers += [(k >= HOP, {"slab": k - HOP}), (k < slabs - HOP, {"slab": k + HOP})]
+    for there, who in peers:
 
         @pl.when(there)
         def _():
-            pl.semaphore_signal(barrier, inc=1, device_id={"energy": energy}, device_id_type=MESH)
-
-    peers = len(always) + 2 - sum((e == end).astype(jnp.int32) for end in (0, energies - 1))
-    pl.semaphore_wait(barrier, peers)
+            pl.semaphore_signal(barrier, inc=1, device_id=who, device_id_type=MESH)
+
+    pl.semaphore_wait(barrier, sum(there.astype(jnp.int32) for there, _ in peers))
 
     def near_copy(slot, target):
         return pltpu.make_async_remote_copy(
@@ -154,10 +183,14 @@
             device_id_type=MESH,
         )
 
-    place = lax.rem(k, HOP)
-    turn = (jnp.where(place == HOP - 1, -HOP, HOP), jnp.where(place == 0, HOP, -HOP))
-    back = (jnp.where(place == 0, HOP, -HOP), jnp.where(place == HOP - 1, -HOP, HOP))
-    beside = (next_k, last_k)
+    sends = [detours(k, way, slabs) for way in range(2)]
+    rides = [relayed(k, way) for way in range(2)]
+    relays = [detours(rides[way], way, slabs) for way in range(2)]
+    handed = [relayed(k + step, way) for way, step in ((0, -1), (1, 1))]
+    hands = [there & detours(handed[way], way, slabs) for way, there in enumerate((has_left, has_right))]
+    gets = [there & detours(k + step, way, slabs) for way, (there, step) in enumerate(((has_left, -1), (has_right, 1)))]
+    beside = (k + 1, k - 1)
+    goes, comes = (has_right, has_left), (has_left, has_right)
     got_v = (from_left_v, from_right_v)
     groups = (DIRECT if around else LIST) // GROUP
     direct, spill, returned, centre = [], [], [], []
@@ -182,7 +215,7 @@
                 spill_v.at[way],
                 spill_send.at[way],
                 spill_recv.at[way],
-                ring(k + turn[way]),
+                k + turned(k, way),
             )
         )
         returned.append(
@@ -191,7 +224,7 @@
                 got_v[way].at[DIRECT:LIST],
                 back_send.at[way],
                 back_recv.at[way],
-                ring(k + back[way]),
+                handed[way] + (1, -1)[way],
             )
         )
         centre.append([])
@@ -210,20 +243,22 @@
         live = (q < count_ref[slab]) & (off_ref[q, slab] == offset)
         return jnp.where(live, range_ref[q, slab], 0)
 
-    def combine(wanted, with_phonon):
+    def combine(wanted, with_phonon, first=0, last=width // TILE):
         reach = [[live_reach(k, q, offset) for q in range(slots)] for _, offset in wanted]
 
         def step(t, carry):
             rows = pl.ds(pl.multiple_of(t * TILE, TILE), TILE)
-            row_ids = t * TILE + lax.broadcasted_iota(jnp.int32, (TILE, width), 0)
             col_ids = lax.broadcasted_iota(jnp.int32, (TILE, width), 1)
-            far = jnp.maximum(row_ids, col_ids)
             m = lax.div(t, UNIT // TILE)
             unit_rows = pl.ds(pl.multiple_of(t * TILE - m * UNIT, TILE), TILE)
+            inside = [
+                [col_ids < jnp.where(t * TILE < reach[n][q], reach[n][q], 0) for q in range(slots)]
+                for n in range(len(wanted))
+            ]
             for part in range(2):
                 terms = [sigma_v[q, part, rows, :].astype(F32) for q in range(slots)]
                 for n, (at, _) in enumerate(wanted):
-                    kept = [jnp.where(far < reach[n][q], terms[q], 0.0) for q in range(slots)]
+                    kept = [jnp.where(inside[n][q], terms[q], 0.0) for q in range(slots)]
                     total = functools.reduce(jnp.add, kept)
                     if with_phonon:
                         low = near_v[0, part, rows, :].astype(F32)
@@ -239,7 +274,7 @@
                             mine_v[at, m, c, unit_rows, lanes] = value
             return carry
 
-        lax.fori_loop(0, width // TILE, step, 0)
+        lax.fori_loop(first, last, step, 0)
 
     def layout(slab, way):
         blocks = []
@@ -267,19 +302,53 @@
 
     for table in tables:
         table.wait()
-    load_sigma.wait()
-    load_green.start()
+    def start(there, *copies):
+        @pl.when(there)
+        def _():
+            for copy in copies:
+                copy.start()
+
+    def arrived(there, *copies):
+        @pl.when(there)
+        def _():
+            for copy in copies:
+                copy.wait_recv()
+
     held_back = groups - 1 if around else groups
-    for way in range(2):
-        combine([(2 * way + n, OFFSETS[2 * way + n]) for n in range(2)], False)
+    tiles = width // TILE // chunks
+    for way in range(2):
+        wanted = [(2 * way + n, OFFSETS[2 * way + n]) for n in range(2)]
+        if way == 0:
+            for c in range(chunks):
+                load_sigma[c].wait()
+                combine(wanted, False, c * tiles, (c + 1) * tiles)
+            load_green.start()
+        else:
+            combine(wanted, False)
         if around:
             pack(way, DIRECT, LIST)
-            spill[way].start()
+            start(sends[way], spill[way])
             pack(way, 0, DIRECT)
         else:
             pack(way, 0, LIST)
-        for copy in direct[way][:held_back]:
-            copy.start()
+        start(goes[way], *direct[way][:held_back])
+
+    for way in range(2):
+
+        @pl.when(jnp.logical_not(comes[way]))
+        def _():
+            got_v[way][...] = jnp.zeros_like(got_v[way])
+            cent_v[way] = jnp.zeros_like(cent_v[way])
+
+        if around:
+
+            @pl.when(comes[way] & jnp.logical_not(gets[way]))
+            def _():
+                got_v[way][DIRECT:LIST] = jnp.zeros_like(got_v[way][DIRECT:LIST])
+
+            @pl.when(jnp.logical_not(relays[way]))
+            def _():
+                spill_v[way] = jnp.zeros_like(spill_v[way])
 
     for there, slot in ((has_low, 0), (has_high, 1)):
 
@@ -298,22 +367,21 @@
     combine([(4, 0)], True)
     if around:
         for way in range(2):
-            spill[way].wait_recv()
+            arrived(relays[way], spill[way])
             for j in range(GROUP):
                 p = DIRECT - GROUP + j
                 list_v[way, p] = list_v[way, p] + spill_v[way, j]
         for way in range(2):
-            direct[way][-1].start()
-    for way in range(2):
-        for copy in centre[way]:
-            copy.start()
+            start(goes[way], direct[way][-1])
+    for way in range(2):
+        start(goes[way], *centre[way])
 
     load_green.wait()
     for at in range(3):
         for part in range(2):
-            turned = green_v[at, part].astype(F32).T
-            plain = turned.astype(BF16)
-            minus = (-turned).astype(BF16)
+            flipped = green_v[at, part].astype(F32).T
+            plain = flipped.astype(BF16)
+            minus = (-flipped).astype(BF16)
             for c in range(chunks):
                 source = slice(c * CHUNK, (c + 1) * CHUNK)
                 real = slice(2 * c * CHUNK, (2 * c + 1) * CHUNK)
@@ -324,7 +392,7 @@
                 else:
                     b_v[at, real, width:] = minus[source]
                     b_v[at, imag, :width] = plain[source]
-    inside = (None, k > 0, k < slabs - 1)
+    inside = (None, has_left, has_right)
     for c in range(chunks):
         for n, at in enumerate((1, 0, 2)):
             for part in range(2):
@@ -368,23 +436,22 @@
 
     if around:
         for way in range(2):
-            direct[way][-1].wait_recv()
-            returned[way].start()
-
-    for way in range(2):
-        for copy in direct[way][:held_back]:
-            copy.wait_recv()
+            arrived(comes[way], direct[way][-1])
+            start(hands[way], returned[way])
+
+    for way in range(2):
+        arrived(comes[way], *direct[way][:held_back])
         if around:
-            returned[way].wait_recv()
-        start = 0
-        blocks = layout((last_k, next_k)[way], way)
+            arrived(gets[way], returned[way])
+        before = 0
+        blocks = layout((jnp.maximum(k - 1, 0), jnp.minimum(k + 1, slabs - 1))[way], way)
         for n, (down_n, across_n, size_n) in enumerate(blocks):
             for m in range(width // UNIT):
                 for c in range(chunks):
-                    position = jnp.clip(start + m * across_n + c, 0, LIST - 1)
+                    position = jnp.clip(before + m * across_n + c, 0, LIST - 1)
                     keep = jnp.where((m < down_n) & (c < across_n), 1.0, 0.0).astype(BF16)
                     block_v[c, m * UNIT : (m + 1) * UNIT] = got_v[way][position] * keep
-            start = start + size_n
+            before = before + size_n
             partner = ((1, 2), (1, 0))[way][n]
             for r in range(chunks):
                 rows = slice(r * CHUNK, (r + 1) * CHUNK)
@@ -398,7 +465,7 @@
         rows = slice(row, row + CHUNK)
         final = n == len(pieces) - 1
         for way in range(2):
-            centre[way][n].wait_recv()
+            arrived(comes[way], centre[way][n])
             partner = (0, 2)[way]
             x = part_v[way, rows]
             for c in range(chunks)[these]:
@@ -424,8 +491,16 @@
         down.wait_send()
 
     for way in range(2):
-        for copy in direct[way] + centre[way] + ([spill[way], returned[way]] if around else []):
-            copy.wait_send()
+        for there, copies in (
+            (goes[way], direct[way] + centre[way]),
+            (sends[way], [spill[way]] if around else []),
+            (hands[way], [returned[way]] if around else []),
+        ):
+
+            @pl.when(there)
+            def _():
+                for copy in copies:
+                    copy.wait_send()
 
 
 def solution(mesh):
@@ -468,7 +543,7 @@
                     pltpu.VMEM((4 * CHUNK, 2 * width), BF16),
                     pltpu.VMEM((2, width, 2 * width), F32),
                     pltpu.VMEM((width, 2 * width), F32),
-                    pltpu.SemaphoreType.DMA((5,)),
+                    pltpu.SemaphoreType.DMA((4 + chunks,)),
                     pltpu.SemaphoreType.DMA((2,)),
                     pltpu.SemaphoreType.DMA((2,)),
                     pltpu.SemaphoreType.DMA((2, LIST // GROUP)),

time: 55.9 us -> 53 us (0.948)
  the two profiles are of different devices: /device:TPU:2 before, /device:TPU:162 now
where the time goes in v1:
time: 53 us; the launch traced here: 52.9 us
  Pallas kernels  50.9 us (96%)
  local copies, waits for them, and re-layouts  1.02 us (2%)
  between operations  0.67 us (1%)
    pallas_call x1, Pallas kernels, call(): pl.pallas_call(functools.partial(kernel, slabs, energies, around), out_sh...  49.5 us
    pallas_call x1, Pallas kernels, body(): pl.pallas_call(crowded_kernel, out_shape=jax.ShapeDtypeStruct((1,), jnp.i...  1.44 us

profile of v1, /device:TPU:162, one launch (start us, length us, event | category | flops | bytes accessed | tf_op | source)
XLA Modules:
  0.0 52.9 jit_solution(1918930865264830124)
XLA Ops:
  0.0 1.4 %crowded.1 = s32[1]{0:T(128)} custom-call(s32[3,32]{1,0:T(4,128)} %bitcast.4, s32[1,32]{1,0:T(1,128)} %bitcast.10, s32[3,32]{1,0:T(4,128)} %bitcast.7), custom_call_target="tpu_custom_call" | custom-call | tf_op jit(solution)/shard_map/crowded/pallas_call | solution.py:564
  2.1 49.7 %conditional.1 = (f32[1,1,2,384,384]{4,3,2,1,0:T(8,128)S(1)}) conditional(s32[]{:T(128)} %bitcast.3, (s32[3,32]{1,0:T(4,128)}, s32[32]{0:T(128)}, s32[3,32]{1,0:T(4,128)}, bf16[1,1,3,2,384,384]{5,4,3,2,1,0:T(8,128)(2,1)}, bf16[1,1,3,2,384,384]{5,4,3,2,1,0:T(8,128)(2,1)}, /*index=5*/bf16[1,1,2,384,384]{4,3,2,1,0:T(8,128)(2,1)}) %tuple.18, ...), branch_computations={%region_0.0_spmd, %region_1.0_spmd} | conditional | bytes 8 | solution.py:571
  2.1 49.5 %around.1 = f32[1,1,2,384,384]{4,3,2,1,0:T(8,128)S(1)} custom-call(s32[3,32]{1,0:T(4,128)} %get-tuple-element.32.off_hbm, s32[32]{0:T(128)} %get-tuple-element.33.count_hbm, s32[3,32]{1,0:T(4,128)} %get-tuple-element.34.range_hbm, bf16[1,1,3,2,384,384]{5,4,3,2,1,0:T(8,128)(2,1)} %get-tuple-element.35.green_hbm, ...), custom_call_target="tpu_custom_call" | custom-call | tf_op jit(solution)/shard_map/cond/branch_0_fun/around/pallas_call | solution.py:521
  51.8 1.0 %copy.12 = f32[1,1,2,384,384]{4,3,2,1,0:T(8,128)} copy(f32[1,1,2,384,384]{4,3,2,1,0:T(8,128)S(1)} %get-tuple-element.44) | data formatting | bytes 2359296
